TPU v7x, 32 devices: a whole 2x2x4 slice. The times are simulated.
32 devices in a mesh: wide: 8 (over z, y), narrow: 4 (over x, core).
Axes of the slice: x: 2, y: 2, z: 4, core: 2. Of those that a mesh axis runs over, the one named last changes fastest.
Arguments:
- noise: bfloat16 [128, 32, 256], P('wide'), may hold values from -6 to 6
- diagonal_tile_blocks: bfloat16 [128, 256, 256], P(('wide', 'narrow')), may hold values from -0.375 to 0.375
- left_factors: bfloat16 [128, 128, 128, 256], P('wide', 'narrow'), may hold values from -0.046875 to 0.046875
- right_factors: bfloat16 [128, 128, 128, 256], P('wide', 'narrow'), may hold values from -0.375 to 0.375
- ranks: int32 [128, 128], P('wide', 'narrow'), may hold values from 0 to 128, as said below
- owner: int32 [128], replicated, may hold values from 0 to 127, as said below
- courant_x: float32 [128, 256], P('wide', 'narrow'), may hold values from 0.05 to 0.4
- courant_number_second: float32 [128, 256], P('wide', 'narrow'), may hold values from 0.05 to 0.4
- upwind_x: int32 [128, 256], P('wide', 'narrow'), may hold values from 0 to 1
- upwind_y: int32 [128, 256], P('wide', 'narrow'), may hold values from 0 to 1
Outputs:
- tracer: float32 [32, 128, 256], P(None, 'wide', 'narrow')
Inputs may be any that keep to these rules, and one draw needn't show every extreme that they name: owner is a permutation of the tile rows 0 to 127. ranks[p, c] is 0 where c >= owner[p] and at least 1 where c < owner[p].
All inputs are finite; a program needn't handle non-finite values.
Results may differ from a plain program's by a relative error of at most 0.0016.
Values may be sent and summed in bfloat16 or wider, within the bound.
A program may use at most 128 MiB of HBM per device.

v0:
```python
import jax
import jax.numpy as jnp
import numpy as np
from jax import lax
from jax.sharding import PartitionSpec as P

TSIDE = 16
TX = 8
TY = 16
ITERS = 4


mixing = 0.05


def with_halo(block, sides, width):
    for axis, dim in sides:
        count = lax.axis_size(axis)
        forward = [(i, i + 1) for i in range(count - 1)]
        forward.append((count - 1, 0))
        backward = [(target, source) for source, target in forward]
        low = lax.ppermute(
            lax.slice_in_dim(block, block.shape[dim] - width, None, axis=dim), axis, forward
        )
        high = lax.ppermute(lax.slice_in_dim(block, 0, width, axis=dim), axis, backward)
        block = jnp.concatenate([low, block, high], axis=dim)
    return block


def morton_table(tiles_x, tiles_y):
    bits_x = tiles_x.bit_length() - 1
    bits_y = tiles_y.bit_length() - 1
    table = np.zeros((tiles_x, tiles_y), np.int32)
    for first in range(tiles_x):
        for second in range(tiles_y):
            morton_code = 0
            position = 0
            for level in range(max(bits_x, bits_y)):
                morton_code = morton_code | (second >> level & 1) << position
                position = position + 1
                if level < bits_x:
                    morton_code = morton_code | (first >> level & 1) << position
                    position = position + 1
            table[first, second] = morton_code
    return table


def advance(
    center, low_x, high_x, low_y, high_y, courant_x, courant_number_second, upwind_x, upwind_y
):
    from_x = jnp.where(upwind_x == 1, low_x, high_x)
    from_y = jnp.where(upwind_y == 1, low_y, high_y)
    return (
        center
        - courant_x * (center - from_x)
        - courant_number_second * (center - from_y)
        + mixing * (low_x + high_x + low_y + high_y - 4.0 * center)
    )


def lookup(indices, table_values):
    total = table_values.shape[0]
    matches = indices[..., None] == jnp.arange(total, dtype=jnp.int32)
    return jnp.sum(jnp.where(matches, table_values, 0), axis=-1)


def per_device(
    noise,
    diagonal_tile_blocks,
    left_factors,
    right_factors,
    ranks,
    owner,
    courant_x,
    courant_number_second,
    upwind_x,
    upwind_y,
):
    all_noise = lax.all_gather(noise, "wide", axis=0, tiled=True)
    col_count = left_factors.shape[1]
    rank_count = left_factors.shape[2]
    col_begin = lax.axis_index("narrow") * col_count
    columns = lax.dynamic_slice_in_dim(all_noise, col_begin, col_count, 0)
    coeff = jnp.einsum("csk,pcrk->pcsr", columns, right_factors, preferred_element_type=jnp.float32)
    levels = lax.broadcasted_iota(jnp.int32, (1, 1, 1, rank_count), 3)
    coeff = jnp.where(levels < ranks[:, :, None, None], coeff, 0.0).astype(jnp.bfloat16)
    partial_value = jnp.einsum(
        "pcsr,pcrk->psk", coeff, left_factors, preferred_element_type=jnp.float32
    )
    row_sums = lax.psum_scatter(partial_value, "narrow", scatter_dimension=0, tiled=True)
    held = row_sums.shape[0]
    device_rank = lax.axis_index("wide") * lax.axis_size("narrow") + lax.axis_index("narrow")
    held_tiles = lax.dynamic_slice_in_dim(owner, device_rank * held, held, 0)
    local_noise_tiles = all_noise[held_tiles]
    diagonal = jnp.einsum(
        "hpg,heg->hpe",
        local_noise_tiles,
        jnp.tril(diagonal_tile_blocks),
        preferred_element_type=jnp.float32,
    )
    samples = row_sums + diagonal
    block_x = courant_x.shape[0]
    block_y = courant_x.shape[1]
    members = samples.shape[1]
    table_np = morton_table(TX, TY)
    whole = lax.all_gather(samples, ("wide", "narrow"), axis=0, tiled=True)
    total_tiles = whole.shape[0]
    inverse_permutation = lookup(
        jnp.asarray(table_np).reshape(-1),
        jnp.zeros((total_tiles,), jnp.int32)
        .at[owner]
        .set(jnp.arange(total_tiles, dtype=jnp.int32)),
    )
    grid = whole[inverse_permutation].reshape(TX, TY, members, TSIDE, TSIDE)
    grid = grid.transpose(2, 0, 3, 1, 4).reshape(members, TX * TSIDE, TY * TSIDE)
    current = lax.dynamic_slice(
        grid,
        (0, lax.axis_index("wide") * block_x, lax.axis_index("narrow") * block_y),
        (members, block_x, block_y),
    )
    stacked = jnp.stack(
        [
            courant_x,
            courant_number_second,
            upwind_x.astype(jnp.float32),
            upwind_y.astype(jnp.float32),
        ]
    )
    padded, coef_padded = (
        with_halo(current, (("wide", 1), ("narrow", 2)), ITERS),
        with_halo(stacked, (("wide", 1), ("narrow", 2)), ITERS),
    )
    flags_x = jnp.where(coef_padded[2] > 0.5, 1, 0)
    flags_y = jnp.where(coef_padded[3] > 0.5, 1, 0)
    for step_index in range(ITERS):
        padded = advance(
            padded,
            jnp.roll(padded, 1, 1),
            jnp.roll(padded, -1, 1),
            jnp.roll(padded, 1, 2),
            jnp.roll(padded, -1, 2),
            coef_padded[0],
            coef_padded[1],
            flags_x,
            flags_y,
        )
    current = padded[:, ITERS : ITERS + block_x, ITERS : ITERS + block_y]
    return current


def solution(mesh):
    placed = (
        P("wide", None, None),
        P(("wide", "narrow"), None, None),
        P("wide", "narrow", None, None),
        P("wide", "narrow", None, None),
        P("wide", "narrow"),
        P(),
        P("wide", "narrow"),
        P("wide", "narrow"),
        P("wide", "narrow"),
        P("wide", "narrow"),
    )
    return jax.shard_map(
        per_device, mesh=mesh, in_specs=placed, out_specs=P(None, "wide", "narrow"), check_vma=False
    )
```

profile of v0, /device:TPU:1, one launch (start us, length us, event | category | flops | bytes accessed | tf_op | source)
XLA Modules:
  0.0 219.9 jit_solution(8425196945456602145)
XLA Ops:
  6.5 0.7 all-gather.3.cloned.1.call-update
  7.3 0.8 iota_compare_fusion.1
  8.2 50.5 %all-gather.3.cloned.1.call-done = bf16[128,32,256]{2,1,0:T(8,128)(2,1)} async-done(((bf16[16,32,256]{2,1,0:T(8,128)(2,1)}), bf16[128,32,256]{2,1,0:T(8,128)(2,1)}) %all-gather.3.cloned.1.call-update) | async-done | bytes 2097168 | tf_op jit(solution)/shard_map/all_gather | solution.py:79
  58.7 25.5 %fusion.5 = f32[16,32,256]{2,1,0:T(8,128)} fusion(bf16[16,32,128,256]{3,2,1,0:T(8,128)(2,1)} %param.13, pred[16,32,128]{2,1,0:T(8,128)(4,1)S(1)} %iota_compare_fusion.1, bf16[16,32,128,256]{3,2,1,0:T(8,128)(2,1)} %param.14, bf16[128,32,256]{2,1,0:T(8,128)(2,1)} %all-gather.3.cloned.1.call-done, s32[]{:T(128)S(6)} %select_n.74), kind=kOutput, calls=%fused_computation.8 | convolution fusion | flops 2151677952 | bytes 68222976 | tf_op jit(solution)/shard_map/pcsr,pcrk->psk/dot_general | solution.py:87
  84.5 2.1 gather_fusion
  86.6 19.8 %reduce-scatter.2.cloned.1.call-done = f32[4,32,256]{2,1,0:T(8,128)} async-done(((f32[16,32,256]{2,1,0:T(8,128)}), f32[4,32,256]{2,1,0:T(8,128)}) %reduce-scatter.2.cloned.1.call-update) | async-done | bytes 131088 | tf_op jit(solution)/shard_map/reduce_scatter | solution.py:90
  106.4 1.8 convolution_add_fusion
  108.3 1.2 collective-permute-start.4
  109.5 3.0 %collective-permute-start.5 = (f32[4,4,64]{2,1,0:T(4,128)S(1)}, f32[4,4,64]{2,1,0:T(4,128)S(1)}, u32[]{:S(2)}, u32[]{:S(2)}) collective-permute-start(f32[4,4,64]{2,1,0:T(4,128)S(1)} %get-tuple-element.46), channel_id=1, source_target_pairs={{4,0},{8,4},{12,8},{16,12},{20,16},{24,20},{28,24},{0,28},{5,1},{9... | collective-permute-start | bytes 12296 | tf_op jit(solution)/shard_map/ppermute | solution.py:25
  112.5 1.0 scatter_custom_fusion
  113.8 1.8 collective-permute-start.6
  115.7 1.1 collective-permute-done.6
  116.8 2.3 %collective-permute-done.7 = f32[4,24,4]{2,1,0:T(8,128)S(1)} collective-permute-done((f32[4,24,4]{2,1,0:T(8,128)S(1)}, f32[4,24,4]{2,1,0:T(8,128)S(1)}, u32[]{:S(2)}, u32[]{:S(2)}) %collective-permute-start.7) | collective-permute-done | bytes 1568 | tf_op jit(solution)/shard_map/ppermute | solution.py:25
  119.2 52.4 %all-gather.5.cloned.1.call-done = f32[128,32,256]{2,1,0:T(8,128)} async-done(((f32[4,32,256]{2,1,0:T(8,128)}), f32[128,32,256]{2,1,0:T(8,128)}) %all-gather.5.cloned.1.call-update) | async-done | bytes 4194320 | tf_op jit(solution)/shard_map/all_gather | solution.py:106
  171.6 5.0 %gather_fusion.1 = f32[128,32,256]{2,1,0:T(8,128)} fusion(f32[128,32,256]{2,1,0:T(8,128)} %all-gather.5.cloned.1.call-done, s32[1024]{0:T(1024)S(1)} %pad_clamp_fusion), kind=kCustom, calls=%fused_computation.1 | custom fusion | bytes 8389120 | tf_op jit(solution)/shard_map/gather | solution.py:114
  176.5 10.3 %copy.29 = f32[128,32,256]{1,2,0:T(8,128)} copy(f32[128,32,256]{2,1,0:T(8,128)} %gather_fusion.1) | data formatting | bytes 8388608 | tf_op jit(solution)/shard_map/gather | solution.py:114
  186.8 7.0 %copy.30 = f32[32,8,16,16,16]{0,4,3,2,1:T(8,128)S(1)} copy(f32[32,8,16,16,16]{0,4,2,3,1:T(8,128)} %bitcast.39) | data formatting | bytes 8388608 | tf_op jit(solution)/shard_map/transpose | solution.py:115
  193.9 1.2 collective-permute-start
  195.1 3.0 %collective-permute-start.1 = (f32[32,4,64]{0,2,1:T(8,128)S(1)}, f32[32,4,64]{0,2,1:T(8,128)S(1)}, u32[]{:S(2)}, u32[]{:S(2)}) collective-permute-start(f32[32,4,64]{0,2,1:T(8,128)S(1)} %get-tuple-element.6), channel_id=1, source_target_pairs={{4,0},{8,4},{12,8},{16,12},{20,16},{24,20},{28,24},{0,28},{5,1},{9... | collective-permute-start | bytes 98312 | tf_op jit(solution)/shard_map/ppermute | solution.py:25
  198.1 3.3 %collective-permute-done = f32[32,4,64]{0,2,1:T(8,128)S(1)} collective-permute-done((f32[32,4,64]{0,2,1:T(8,128)S(1)}, f32[32,4,64]{0,2,1:T(8,128)S(1)}, u32[]{:S(2)}, u32[]{:S(2)}) %collective-permute-start) | collective-permute-done | bytes 32800 | tf_op jit(solution)/shard_map/ppermute | solution.py:22
  201.4 1.0 collective-permute-done.1
  202.5 2.0 collective-permute-start.2
  206.0 2.1 collective-permute-done.3
  212.1 1.3 multiply_add_fusion.3
  (73 shorter events, 6.3 us)
Async XLA Ops:
  6.5 52.2 %all-gather.3.cloned.1.call-start = ((), (), s32[]{:S(2)}) async-start(), calls=%async_computation.1 | async-start | bytes 2359296 | tf_op jit(solution)/shard_map/all_gather | solution.py:79
  7.3 99.1 %reduce-scatter.2.cloned.1.call-start = ((), (), s32[]{:S(2)}) async-start(), calls=%async_computation.2 | async-start | bytes 655360 | tf_op jit(solution)/shard_map/reduce_scatter | solution.py:90
  8.1 76.2 %copy-start.5 = (s32[128]{0:T(128)S(1)}, s32[128]{0:T(128)}, u32[]{:S(2)}) copy-start(s32[128]{0:T(128)} %param.16) | copy-start | bytes 1540
  8.2 98.2 %copy-start.4 = (bf16[4,256,256]{2,1,0:T(8,128)(2,1)S(1)}, bf16[4,256,256]{2,1,0:T(8,128)(2,1)}, u32[]{:S(2)}) copy-start(bf16[4,256,256]{2,1,0:T(8,128)(2,1)} %param.12) | copy-start | bytes 1572868
  8.2 100.1 %copy-start.2 = (s32[16,64]{1,0:T(8,128)S(1)}, s32[16,64]{1,0:T(8,128)}, u32[]{:S(2)}) copy-start(s32[16,64]{1,0:T(8,128)} %param.20) | copy-start | bytes 12292
  8.2 100.1 %copy-start.3 = (s32[16,64]{1,0:T(8,128)S(1)}, s32[16,64]{1,0:T(8,128)}, u32[]{:S(2)}) copy-start(s32[16,64]{1,0:T(8,128)} %param.19) | copy-start | bytes 12292
  8.2 100.1 %copy-start = (f32[16,64]{1,0:T(8,128)S(1)}, f32[16,64]{1,0:T(8,128)}, u32[]{:S(2)}) copy-start(f32[16,64]{1,0:T(8,128)} %param.18) | copy-start | bytes 12292
  8.2 100.1 %copy-start.1 = (f32[16,64]{1,0:T(8,128)S(1)}, f32[16,64]{1,0:T(8,128)}, u32[]{:S(2)}) copy-start(f32[16,64]{1,0:T(8,128)} %param.17) | copy-start | bytes 12292
  8.2 105.3 %copy-start.6 = (s32[128]{0:T(128)S(1)}, s32[128]{0:T(128)}, u32[]{:S(2)}) copy-start(s32[128]{0:T(128)} %constant.45) | copy-start | bytes 1540
  84.3 87.3 %all-gather.5.cloned.1.call-start = ((), (), s32[]{:S(2)}) async-start(), calls=%async_computation.3 | async-start | bytes 4325376 | tf_op jit(solution)/shard_map/all_gather | solution.py:106
  108.3 5.4 %collective-permute-start.4 = (f32[4,4,64]{2,1,0:T(4,128)S(1)}, f32[4,4,64]{2,1,0:T(4,128)S(1)}, u32[]{:S(2)}, u32[]{:S(2)}) collective-permute-start(f32[4,4,64]{2,1,0:T(4,128)S(1)} %get-tuple-element.45), channel_id=1, source_target_pairs={{0,4},{4,8},{8,12},{12,16},{16,20},{20,24},{24,28},{28,0},{1,5},{5... | collective-permute-start | bytes 12296 | tf_op jit(solution)/shard_map/ppermute | solution.py:22
  109.5 4.2 %collective-permute-start.5 = (f32[4,4,64]{2,1,0:T(4,128)S(1)}, f32[4,4,64]{2,1,0:T(4,128)S(1)}, u32[]{:S(2)}, u32[]{:S(2)}) collective-permute-start(f32[4,4,64]{2,1,0:T(4,128)S(1)} %get-tuple-element.46), channel_id=1, source_target_pairs={{4,0},{8,4},{12,8},{16,12},{20,16},{24,20},{28,24},{0,28},{5,1},{9... | collective-permute-start | bytes 12296 | tf_op jit(solution)/shard_map/ppermute | solution.py:25
  113.8 2.9 %collective-permute-start.6 = (f32[4,24,4]{2,1,0:T(8,128)S(1)}, f32[4,24,4]{2,1,0:T(8,128)S(1)}, u32[]{:S(2)}, u32[]{:S(2)}) collective-permute-start(f32[4,24,4]{2,1,0:T(8,128)S(1)} %get-tuple-element.43), channel_id=1, source_target_pairs={{0,1},{1,2},{2,3},{3,0},{4,5},{5,6},{6,7},{7,4},{8,9},{9,10},{10,1... | collective-permute-start | bytes 4616 | tf_op jit(solution)/shard_map/ppermute | solution.py:22
  115.6 3.5 %collective-permute-start.7 = (f32[4,24,4]{2,1,0:T(8,128)S(1)}, f32[4,24,4]{2,1,0:T(8,128)S(1)}, u32[]{:S(2)}, u32[]{:S(2)}) collective-permute-start(f32[4,24,4]{2,1,0:T(8,128)S(1)} %get-tuple-element.44), channel_id=1, source_target_pairs={{1,0},{2,1},{3,2},{0,3},{5,4},{6,5},{7,6},{4,7},{9,8},{10,9},{11,1... | collective-permute-start | bytes 4616 | tf_op jit(solution)/shard_map/ppermute | solution.py:25
  193.9 7.5 %collective-permute-start = (f32[32,4,64]{0,2,1:T(8,128)S(1)}, f32[32,4,64]{0,2,1:T(8,128)S(1)}, u32[]{:S(2)}, u32[]{:S(2)}) collective-permute-start(f32[32,4,64]{0,2,1:T(8,128)S(1)} %get-tuple-element.5), channel_id=1, source_target_pairs={{0,4},{4,8},{8,12},{12,16},{16,20},{20,24},{24,28},{28,0},{1,5},{5... | collective-permute-start | bytes 98312 | tf_op jit(solution)/shard_map/ppermute | solution.py:22
  195.1 7.3 %collective-permute-start.1 = (f32[32,4,64]{0,2,1:T(8,128)S(1)}, f32[32,4,64]{0,2,1:T(8,128)S(1)}, u32[]{:S(2)}, u32[]{:S(2)}) collective-permute-start(f32[32,4,64]{0,2,1:T(8,128)S(1)} %get-tuple-element.6), channel_id=1, source_target_pairs={{4,0},{8,4},{12,8},{16,12},{20,16},{24,20},{28,24},{0,28},{5,1},{9... | collective-permute-start | bytes 98312 | tf_op jit(solution)/shard_map/ppermute | solution.py:25
  202.5 3.2 %collective-permute-start.2 = (f32[32,24,4]{0,2,1:T(4,128)S(1)}, f32[32,24,4]{0,2,1:T(4,128)S(1)}, u32[]{:S(2)}, u32[]{:S(2)}) collective-permute-start(f32[32,24,4]{0,2,1:T(4,128)S(1)} %get-tuple-element.7), channel_id=1, source_target_pairs={{0,1},{1,2},{2,3},{3,0},{4,5},{5,6},{6,7},{7,4},{8,9},{9,10},{10,1... | collective-permute-start | bytes 36872 | tf_op jit(solution)/shard_map/ppermute | solution.py:22
  204.5 3.5 %collective-permute-start.3 = (f32[32,24,4]{0,2,1:T(4,128)S(1)}, f32[32,24,4]{0,2,1:T(4,128)S(1)}, u32[]{:S(2)}, u32[]{:S(2)}) collective-permute-start(f32[32,24,4]{0,2,1:T(4,128)S(1)} %get-tuple-element.8), channel_id=1, source_target_pairs={{1,0},{2,1},{3,2},{0,3},{5,4},{6,5},{7,6},{4,7},{9,8},{10,9},{11,1... | collective-permute-start | bytes 36872 | tf_op jit(solution)/shard_map/ppermute | solution.py:25
Sparse Core Ops, SparseCore 0:
  9.5 49.2 all-gather.2
  84.4 21.9 reduce-scatter.1
  109.2 62.2 all-gather.4
where the time goes:
time: 220 us
  waiting for transfers between devices  134 us (61%)
  local copies, waits for them, and re-layouts  28.8 us (13%)
  matrix products  27.4 us (12%)
  between operations  13.5 us (6%)
  starting transfers between devices  12.4 us (6%)
  other arithmetic  4.21 us (2%)
    all_gather x1, waiting for transfers between devices, per_device(): whole = lax.all_gather(samples, ('wide', 'narrow'), axis=0, tiled=True)  52.4 us
    all_gather x1, waiting for transfers between devices, per_device(): all_noise = lax.all_gather(noise, 'wide', axis=0, tiled=True)  50.5 us
    dot_general x1, matrix products, per_device(): jnp.einsum('pcsr,pcrk->psk', coeff, left_factors, preferred_element_type=...  25.5 us
    reduce_scatter x1, waiting for transfers between devices, per_device(): lax.psum_scatter(partial_value, 'narrow', scatter_dimension=0, tiled=True)  19.8 us
    gather x2, local copies, waits for them, and re-layouts, per_device(): grid = whole[inverse_permutation].reshape(TX, TY, members, TSIDE, TSIDE)  15.3 us
    transpose x1, local copies, waits for them, and re-layouts, per_device(): grid.transpose(2, 0, 3, 1, 4).reshape(members, TX * TSIDE, TY * TSIDE)  7.01 us
    ppermute x4, starting transfers between devices, with_halo(): lax.ppermute(lax.slice_in_dim(block, block.shape[dim] - width, None, axis...  6.24 us
    ppermute x4, starting transfers between devices, with_halo(): lax.ppermute(lax.slice_in_dim(block, 0, width, axis=dim), axis, backward)  6.04 us
  transfers between devices with their start and end apart: 11, of which 9 were waited for; matrix products, arithmetic and copies ran while one was open for 2% of the time, Pallas kernels for 0%

commit v1 on v0

v1 whole, which is shorter than its diff:
```python
import functools

import jax
import jax.numpy as jnp
import numpy as np
from jax import lax
from jax.experimental import pallas as pl
from jax.experimental.pallas import tpu as pltpu
from jax.sharding import PartitionSpec as P

TSIDE = 16
TX = 8
TY = 16
ITERS = 4
MESH = pl.DeviceIdType.MESH
VMEM = pltpu.VMEM
SMEM = pltpu.SMEM
HALVES = 2


mixing = 0.05


def morton_table(tiles_x, tiles_y):
    bits_x = tiles_x.bit_length() - 1
    bits_y = tiles_y.bit_length() - 1
    table = np.zeros((tiles_x, tiles_y), np.int32)
    for first in range(tiles_x):
        for second in range(tiles_y):
            morton_code = 0
            position = 0
            for level in range(max(bits_x, bits_y)):
                if level < bits_y:
                    morton_code = morton_code | (second >> level & 1) << position
                    position = position + 1
                if level < bits_x:
                    morton_code = morton_code | (first >> level & 1) << position
                    position = position + 1
            table[first, second] = morton_code
    return table


def advance(
    center, low_x, high_x, low_y, high_y, courant_x, courant_number_second, upwind_x, upwind_y
):
    from_x = jnp.where(upwind_x == 1, low_x, high_x)
    from_y = jnp.where(upwind_y == 1, low_y, high_y)
    return (
        center
        - courant_x * (center - from_x)
        - courant_number_second * (center - from_y)
        + mixing * (low_x + high_x + low_y + high_y - 4.0 * center)
    )


def remote(src, dst, send_sem, recv_sem, device):
    return pltpu.make_async_remote_copy(
        src_ref=src,
        dst_ref=dst,
        send_sem=send_sem,
        recv_sem=recv_sem,
        device_id=device,
        device_id_type=MESH,
    )


def spread_kernel(
    wides,
    narrows,
    noise_ref,
    coef_ref,
    owner_ref,
    diag_ref,
    cols_ref,
    diag_out_ref,
    coefs_ref,
    picked,
    picked_in,
    noise_send,
    noise_recv,
    pass_send,
    own_sem,
    coef_send,
    coef_recv,
    own_coef_sem,
    pick_send,
    pick_recv,
):
    w = lax.axis_index("wide")
    n = lax.axis_index("narrow")
    tiles = noise_ref.shape[0]
    held = diag_ref.shape[0]
    cells = diag_ref.shape[1]
    cols = cols_ref.shape[0]
    ratio = wides // narrows
    line = wides // 2
    part = tiles // HALVES
    parity = lax.rem(w, 2)
    partner = w + 1 - 2 * parity
    place = lax.rem(w, ratio)
    is_source = w // ratio == n

    def columns(block, half):
        return cols_ref.at[pl.ds(block * tiles + half * part, part)]

    def noise_copy(step, half):
        target = parity + 2 * lax.rem(w // 2 + step, line)
        return remote(
            noise_ref.at[pl.ds(half * part, part)],
            columns(place, half),
            noise_send.at[step, half],
            noise_recv.at[place, half],
            (target, n),
        )

    own_copy = pltpu.make_async_copy(
        noise_ref, cols_ref.at[pl.ds(place * tiles, tiles)], own_sem
    )

    @pl.when(is_source)
    def _():
        for half in range(HALVES):
            for step in range(1, line):
                noise_copy(step, half).start()
        own_copy.start()

    def coef_copy(slot, step):
        target = (lax.rem(w + 1 - slot + wides, wides), lax.rem(n + step, narrows))
        return remote(
            coef_ref,
            coefs_ref.at[slot, n],
            coef_send.at[slot, step],
            coef_recv.at[slot, step],
            target,
        )

    for slot in range(3):
        for step in range(narrows):
            if slot != 1 or step != 0:
                coef_copy(slot, step).start()
    own_coef = pltpu.make_async_copy(coef_ref, coefs_ref.at[1, n], own_coef_sem)
    own_coef.start()

    def pass_copy(pair, half):
        block = 2 * pair + parity
        return remote(
            columns(block, half),
            columns(block, half),
            pass_send.at[pair, half],
            noise_recv.at[block, half],
            (partner, n),
        )

    def arrival(block, half):
        return remote(
            columns(block, half),
            columns(block, half),
            pass_send.at[0, half],
            noise_recv.at[block, half],
            (partner, n),
        )

    @pl.when(is_source)
    def _():
        own_copy.wait()

    for half in range(HALVES):
        for pair in range(ratio // 2):
            block = 2 * pair + parity

            @pl.when(w != ratio * n + block)
            def _():
                arrival(block, half).wait_recv()

            pass_copy(pair, half).start()
    for half in range(HALVES):
        for pair in range(ratio // 2):
            arrival(2 * pair + 1 - parity, half).wait_recv()

    for k in range(narrows):
        for h in range(held):
            tile = owner_ref[w * (narrows * held) + k * held + h] - n * cols
            inside = jnp.where((tile >= 0) & (tile < cols), 1.0, 0.0).astype(jnp.float32)
            block = cols_ref[jnp.clip(tile, 0, cols - 1)]
            picked[k, h] = (block.astype(jnp.float32) * inside).astype(jnp.bfloat16)

    def pick_copy(step):
        k = lax.rem(n + step, narrows)
        return remote(
            picked.at[k], picked_in.at[n], pick_send.at[step], pick_recv.at[step], (w, k)
        )

    for step in range(1, narrows):
        pick_copy(step).start()
    total = picked[n].astype(jnp.float32)
    for step in range(1, narrows):
        pick_copy(step).wait_recv()
    for step in range(1, narrows):
        total = total + picked_in[lax.rem(n - step + narrows, narrows)].astype(jnp.float32)
    row = lax.broadcasted_iota(jnp.int32, (cells, cells), 0)
    col = lax.broadcasted_iota(jnp.int32, (cells, cells), 1)
    for h in range(held):
        lower = jnp.where(col <= row, diag_ref[h].astype(jnp.float32), 0.0).astype(jnp.bfloat16)
        diag_out_ref[h] = lax.dot_general(
            total[h].astype(jnp.bfloat16),
            lower,
            (((1,), (1,)), ((), ())),
            preferred_element_type=jnp.float32,
        )

    for step in range(1, narrows):
        pick_copy(step).wait_send()
    own_coef.wait()
    for slot in range(3):
        for step in range(narrows):
            if slot != 1 or step != 0:
                coef_copy(slot, step).wait()
    for half in range(HALVES):
        for pair in range(ratio // 2):
            pass_copy(pair, half).wait_send()

    @pl.when(is_source)
    def _():
        for half in range(HALVES):
            for step in range(1, line):
                noise_copy(step, half).wait_send()


def spread(wides, narrows, noise, coef, owner, diag):
    tiles, members, cells = noise.shape
    held = diag.shape[0]
    ratio = wides // narrows
    line = wides // 2
    dma = pltpu.SemaphoreType.DMA
    vmem = pl.BlockSpec(memory_space=VMEM)
    return pl.pallas_call(
        functools.partial(spread_kernel, wides, narrows),
        name="spread",
        out_shape=(
            jax.ShapeDtypeStruct((ratio * tiles, members, cells), jnp.bfloat16),
            jax.ShapeDtypeStruct((held, members, cells), jnp.float32),
            jax.ShapeDtypeStruct((3, narrows) + coef.shape, jnp.float32),
        ),
        in_specs=[vmem, vmem, pl.BlockSpec(memory_space=SMEM), vmem],
        out_specs=(vmem, vmem, vmem),
        scratch_shapes=[
            pltpu.VMEM((narrows, held, members, cells), jnp.bfloat16),
            pltpu.VMEM((narrows, held, members, cells), jnp.bfloat16),
            dma((line, HALVES)),
            dma((ratio, HALVES)),
            dma((max(ratio // 2, 1), HALVES)),
            dma,
            dma((3, narrows)),
            dma((3, narrows)),
            dma,
            dma((narrows,)),
            dma((narrows,)),
        ],
        compiler_params=pltpu.CompilerParams(has_side_effects=True),
    )(noise, coef, owner, diag)


def rows_kernel(
    narrows, ranks_ref, cols_ref, diag_ref, left_ref, right_ref, out_ref, coeff_ref
):
    p = pl.program_id(0)
    n = lax.axis_index("narrow")
    cols = cols_ref.shape[0]
    members = cols_ref.shape[1]
    rank = right_ref.shape[2]
    held = diag_ref.shape[0]
    level = lax.broadcasted_iota(jnp.int32, (members, rank), 1)
    for c in range(cols):
        coeff = lax.dot_general(
            cols_ref[c],
            right_ref[0, c],
            (((1,), (1,)), ((), ())),
            preferred_element_type=jnp.float32,
        )
        coeff = jnp.where(level < ranks_ref[p, c], coeff, 0.0).astype(jnp.bfloat16)
        coeff_ref[:, c * rank : (c + 1) * rank] = coeff
    left = left_ref[0].reshape(cols * rank, left_ref.shape[3])
    total = jnp.dot(coeff_ref[...], left, preferred_element_type=jnp.float32)
    at = p - n * held
    mine = jnp.where((at >= 0) & (at < held), 1.0, 0.0).astype(jnp.float32)
    total = total + mine * diag_ref[jnp.clip(at, 0, held - 1)]
    group = members // narrows
    for k in range(narrows):
        out_ref[k, 0] = total[k * group : (k + 1) * group]


def row_sums(narrows, ranks, cols, diag, left, right):
    rows, count, rank, cells = left.shape
    members = cols.shape[1]
    group = members // narrows
    factor = pl.BlockSpec((1, count, rank, cells), lambda p: (p, 0, 0, 0))
    return pl.pallas_call(
        functools.partial(rows_kernel, narrows),
        name="row_sums",
        grid=(rows,),
        out_shape=jax.ShapeDtypeStruct((narrows, rows, group, cells), jnp.float32),
        in_specs=[
            pl.BlockSpec(memory_space=SMEM),
            pl.BlockSpec(cols.shape, lambda p: (0, 0, 0)),
            pl.BlockSpec(diag.shape, lambda p: (0, 0, 0)),
            factor,
            factor,
        ],
        out_specs=pl.BlockSpec((narrows, 1, group, cells), lambda p: (0, p, 0, 0)),
        scratch_shapes=[pltpu.VMEM((members, count * rank), jnp.bfloat16)],
    )(ranks, cols, diag, left, right)


def share_kernel(
    wides,
    narrows,
    part_ref,
    all_ref,
    came,
    part_send,
    part_recv,
    line_send,
    line_recv,
    pass_send,
    pass_recv,
):
    w = lax.axis_index("wide")
    n = lax.axis_index("narrow")
    size = part_ref.shape[1] // HALVES
    line = wides // 2
    parity = lax.rem(w, 2)
    partner = w + 1 - 2 * parity

    def part_copy(step, half):
        k = lax.rem(n + step, narrows)
        rows = pl.ds(half * size, size)
        return remote(
            part_ref.at[k, rows],
            came.at[n, rows],
            part_send.at[step, half],
            part_recv.at[step, half],
            (w, k),
        )

    def line_copy(step, half):
        target = parity + 2 * lax.rem(w // 2 + step, line)
        block = all_ref.at[w, pl.ds(half * size, size)]
        return remote(
            block, block, line_send.at[step, half], line_recv.at[step, half], (target, n)
        )

    def pass_copy(step, half):
        source = parity + 2 * lax.rem(w // 2 - step + line, line)
        block = all_ref.at[source, pl.ds(half * size, size)]
        return remote(
            block, block, pass_send.at[step, half], pass_recv.at[step, half], (partner, n)
        )

    for half in range(HALVES):
        for step in range(1, narrows):
            part_copy(step, half).start()
    for half in range(HALVES):
        for step in range(1, narrows):
            part_copy(step, half).wait_recv()
        rows = pl.ds(half * size, size)
        total = part_ref[n, rows]
        for step in range(1, narrows):
            total = total + came[lax.rem(n - step + narrows, narrows), rows]
        all_ref[w, rows] = total
        for step in range(1, line):
            line_copy(step, half).start()
        pass_copy(0, half).start()
    for half in range(HALVES):
        for step in range(1, line):
            line_copy(step, half).wait_recv()
            pass_copy(step, half).start()
    for half in range(HALVES):
        for step in range(line):
            pass_copy(step, half).wait()
        for step in range(1, line):
            line_copy(step, half).wait_send()
        for step in range(1, narrows):
            part_copy(step, half).wait_send()


def share(wides, narrows, part):
    line = wides // 2
    dma = pltpu.SemaphoreType.DMA
    vmem = pl.BlockSpec(memory_space=VMEM)
    return pl.pallas_call(
        functools.partial(share_kernel, wides, narrows),
        name="share",
        out_shape=jax.ShapeDtypeStruct((wides,) + part.shape[1:], jnp.float32),
        in_specs=[vmem],
        out_specs=vmem,
        scratch_shapes=[
            pltpu.VMEM(part.shape, jnp.float32),
            dma((narrows, HALVES)),
            dma((narrows, HALVES)),
            dma((line, HALVES)),
            dma((line, HALVES)),
            dma((line, HALVES)),
            dma((line, HALVES)),
        ],
        compiler_params=pltpu.CompilerParams(has_side_effects=True),
    )(part)


def exchange_kernel(narrows, in_ref, out_ref, own_sem, send, recv):
    w = lax.axis_index("wide")
    n = lax.axis_index("narrow")

    def copy(step):
        k = lax.rem(n + step, narrows)
        return remote(in_ref.at[k], out_ref.at[n], send.at[step], recv.at[step], (w, k))

    for step in range(1, narrows):
        copy(step).start()
    own = pltpu.make_async_copy(in_ref.at[n], out_ref.at[n], own_sem)
    own.start()
    own.wait()
    for step in range(1, narrows):
        copy(step).wait()


def exchange(narrows, blocks):
    dma = pltpu.SemaphoreType.DMA
    vmem = pl.BlockSpec(memory_space=VMEM)
    return pl.pallas_call(
        functools.partial(exchange_kernel, narrows),
        name="exchange",
        out_shape=jax.ShapeDtypeStruct(blocks.shape, jnp.float32),
        in_specs=[vmem],
        out_specs=vmem,
        scratch_shapes=[dma, dma((narrows,)), dma((narrows,))],
        compiler_params=pltpu.CompilerParams(has_side_effects=True),
    )(blocks)


def per_device(
    noise,
    diagonal_tile_blocks,
    left_factors,
    right_factors,
    ranks,
    owner,
    courant_x,
    courant_number_second,
    upwind_x,
    upwind_y,
):
    wides = lax.axis_size("wide")
    narrows = lax.axis_size("narrow")
    w = lax.axis_index("wide")
    block_x, block_y = courant_x.shape
    coef = jnp.stack(
        [
            courant_x,
            courant_number_second,
            upwind_x.astype(jnp.float32),
            upwind_y.astype(jnp.float32),
        ]
    )
    cols, diag, coefs = spread(wides, narrows, noise, coef, owner, diagonal_tile_blocks)
    part = row_sums(narrows, ranks, cols, diag, left_factors, right_factors)
    whole = share(wides, narrows, part)
    group, cells = whole.shape[2:]
    total_tiles = wides * whole.shape[1]
    whole = whole.reshape(total_tiles, group, cells)

    height = block_x + 2 * ITERS
    width = TY * TSIDE
    first = w * block_x - ITERS + TX * TSIDE
    first_tile = first // TSIDE
    tile_rows = (height + 2 * TSIDE - 1 - ITERS) // TSIDE
    table = jnp.asarray(morton_table(TX, TY))
    wanted = table[(first_tile + jnp.arange(tile_rows)) % TX].reshape(-1)
    matches = wanted[:, None] == owner[None, :]
    stored = jnp.sum(
        jnp.where(matches, jnp.arange(total_tiles, dtype=jnp.int32)[None, :], 0), axis=1
    )
    field = whole[stored].reshape(tile_rows, TY, group, TSIDE, TSIDE)
    field = field.transpose(2, 0, 3, 1, 4).reshape(group, tile_rows * TSIDE, width)
    field = lax.dynamic_slice_in_dim(field, first - first_tile * TSIDE, height, 1)
    coefs = coefs.transpose(2, 0, 3, 1, 4).reshape(4, 3 * block_x, width)
    coefs = coefs[:, block_x - ITERS : 2 * block_x + ITERS]
    flags_x = jnp.where(coefs[2] > 0.5, 1, 0)
    flags_y = jnp.where(coefs[3] > 0.5, 1, 0)
    for step_index in range(ITERS):
        field = advance(
            field,
            jnp.roll(field, 1, 1),
            jnp.roll(field, -1, 1),
            jnp.roll(field, 1, 2),
            jnp.roll(field, -1, 2),
            coefs[0],
            coefs[1],
            flags_x,
            flags_y,
        )
    field = field[:, ITERS : ITERS + block_x]
    field = field.reshape(group, block_x, narrows, block_y).transpose(2, 0, 1, 3)
    return exchange(narrows, field).reshape(narrows * group, block_x, block_y)


def solution(mesh):
    placed = (
        P("wide", None, None),
        P(("wide", "narrow"), None, None),
        P("wide", "narrow", None, None),
        P("wide", "narrow", None, None),
        P("wide", "narrow"),
        P(),
        P("wide", "narrow"),
        P("wide", "narrow"),
        P("wide", "narrow"),
        P("wide", "narrow"),
    )
    return jax.shard_map(
        per_device, mesh=mesh, in_specs=placed, out_specs=P(None, "wide", "narrow"), check_vma=False
    )
```

time: 220 us -> 129 us (0.59)
  waiting for transfers between devices: 134 us -> 0 us
  Pallas kernels: 0 us -> 104 us
  matrix products: 27.4 us -> 0 us
  between operations: 13.5 us -> 0.24 us
  starting transfers between devices: 12.4 us -> 0 us
  local copies, waits for them, and re-layouts: 28.8 us -> 16.9 us
  other arithmetic: 4.21 us -> 6.73 us
    pallas_call x0 -> x4, Pallas kernels: none -> 104 us  [the longest x1 35.2 us: spread(): pl.pallas_call(functools.partial(spread_kernel, wides, narrows), name='sp...]
    all_gather x2 -> x0, waiting for transfers between devices: 103 us -> none  [the longest x1 52.4 us: per_device(): whole = lax.all_gather(samples, ('wide', 'narrow'), axis=0, tiled=True)]
    dot_general x2 -> x0, matrix products: 27.4 us -> none  [the longest x1 25.5 us: per_device(): jnp.einsum('pcsr,pcrk->psk', coeff, left_factors, preferred_element_type=...]
    reduce_scatter x1 -> x0, waiting for transfers between devices: 19.8 us -> none  [per_device(): lax.psum_scatter(partial_value, 'narrow', scatter_dimension=0, tiled=True)]
    gather x3 -> x2, local copies, waits for them, and re-layouts: 17.4 us -> 3.05 us  [the longest x1 1.81 us: per_device(): field = whole[stored].reshape(tile_rows, TY, group, TSIDE, TSIDE)]
    ppermute x8 -> x0, starting transfers between devices: 12.3 us -> none  [the longest x4 6.24 us: with_halo(): lax.ppermute(lax.slice_in_dim(block, block.shape[dim] - width, None, axis...]
    ppermute x8 -> x0, waiting for transfers between devices: 10.4 us -> none  [the longest x4 5.46 us: with_halo(): lax.ppermute(lax.slice_in_dim(block, 0, width, axis=dim), axis, backward)]
    reshape x0 -> x5, local copies, waits for them, and re-layouts: none -> 4.91 us  [the longest x1 2.8 us: per_device(): field.transpose(2, 0, 3, 1, 4).reshape(group, tile_rows * TSIDE, width)]
  transfers between devices with their start and end apart: 11 -> 0, of which waited for: 9 -> 0; matrix products, arithmetic and copies ran while one was open for 2% -> 0% of each run, Pallas kernels for 0% -> 0%
where the time goes in v1:
time: 129 us; the launch traced here: 128 us
  Pallas kernels  104 us (81%)
  local copies, waits for them, and re-layouts  16.9 us (13%)
  other arithmetic  6.73 us (5%)
    pallas_call x1, Pallas kernels, spread(): pl.pallas_call(functools.partial(spread_kernel, wides, narrows), name='sp...  35.2 us
    pallas_call x1, Pallas kernels, row_sums(): pl.pallas_call(functools.partial(rows_kernel, narrows), name='row_sums',...  30.8 us
    pallas_call x1, Pallas kernels, share(): pl.pallas_call(functools.partial(share_kernel, wides, narrows), name='sha...  27.6 us
    pallas_call x1, Pallas kernels, exchange(): pl.pallas_call(functools.partial(exchange_kernel, narrows), name='exchang...  10.4 us
    add x4, other arithmetic, advance(): center - courant_x * (center - from_x)  3.8 us
    transpose x1, local copies, waits for them, and re-layouts, per_device(): field.transpose(2, 0, 3, 1, 4).reshape(group, tile_rows * TSIDE, width)  3.48 us
    reshape x1, local copies, waits for them, and re-layouts, per_device(): field.transpose(2, 0, 3, 1, 4).reshape(group, tile_rows * TSIDE, width)  2.8 us

profile of v1, /device:TPU:1, one launch (start us, length us, event | category | flops | bytes accessed | tf_op | source)
XLA Modules:
  0.0 127.9 jit_solution(13270305326244256477)
XLA Ops:
  0.0 1.2 gather_fusion
  1.4 0.8 select_reduce_fusion
  2.2 0.7 convert_bitcast_fusion
  2.9 1.3 %pad_maximum_fusion.14.coef_ref = f32[4,16,64]{2,1,0:T(8,128)} fusion(f32[1,16,64]{2,1,0:T(8,128)S(1)} %get-tuple-element.47, f32[1,16,64]{2,1,0:T(8,128)S(1)} %get-tuple-element.48, f32[1,16,64]{2,1,0:T(8,128)} %bitcast.34, f32[1,16,64]{2,1,0:T(8,128)} %bitcast.35), kind=kLoop, calls=%fused_computation.27 | loop fusion | flops 12288 | bytes 32768 | tf_op jit(solution)/shard_map/stack | solution.py:456
  4.3 35.2 %spread.1 = (bf16[32,32,256]{2,1,0:T(8,128)(2,1)}, f32[4,32,256]{2,1,0:T(8,128)}, f32[3,4,4,16,64]{4,3,2,1,0:T(8,128)}) custom-call(bf16[16,32,256]{2,1,0:T(8,128)(2,1)} %noise_ref.1, f32[4,16,64]{2,1,0:T(8,128)} %pad_maximum_fusion.14.coef_ref, s32[128]{0:T(128)} %owner_ref.1, bf16[4,256,256]{2,1,0:T(8,128)(2,1)} %diag_ref.1), custom_call_target="tpu_custom_call" | custom-call | tf_op jit(solution)/shard_map/spread/pallas_call | solution.py:236
  39.5 30.8 %row_sums.1.part_ref = f32[4,16,8,256]{3,2,1,0:T(8,128)} custom-call(s32[16,32]{1,0:T(8,128)} %ranks_ref.1, bf16[32,32,256]{2,1,0:T(8,128)(2,1)} %get-tuple-element.8.cols_ref, f32[4,32,256]{2,1,0:T(8,128)} %get-tuple-element.9.diag_ref, bf16[16,32,128,256]{3,2,1,0:T(8,128)(2,1)} %left_ref.1, bf16[16,32,128,256]{3,2,1,0:T(8,128)(2,1)} %right_ref.1), custom_call_target="tpu_custom_call" | custom-call | tf_op jit(solution)/shard_map/row_sums/pallas_call | solution.py:297
  70.3 0.3 copy.18
  70.6 0.3 reshape.99
  70.9 0.6 slice.199
  71.5 0.6 slice.205
  72.1 0.6 slice.206
  72.7 0.6 slice.207
  73.3 27.6 %share.1 = f32[8,16,8,256]{3,2,1,0:T(8,128)} custom-call(f32[4,16,8,256]{3,2,1,0:T(8,128)} %row_sums.1.part_ref), custom_call_target="tpu_custom_call" | custom-call | tf_op jit(solution)/shard_map/share/pallas_call | solution.py:390
  100.9 1.8 %gather_fusion.1 = f32[48,8,256]{2,1,0:T(8,128)S(1)} fusion(f32[128,8,256]{2,1,0:T(8,128)} %bitcast.30, s32[1024]{0:T(1024)S(1)} %pad_clamp_fusion), kind=kCustom, calls=%fused_computation.1 | custom fusion | bytes 786624 | tf_op jit(solution)/shard_map/gather | solution.py:482
  102.7 1.0 reshape.97
  103.7 3.5 %copy.17 = f32[8,3,16,16,16]{4,3,2,1,0:T(8,128)} copy(f32[8,3,16,16,16]{4,2,0,3,1:T(8,128)S(1)} %bitcast.29) | data formatting | bytes 786432 | tf_op jit(solution)/shard_map/transpose | solution.py:483
  107.2 2.8 %reshape.98 = f32[8,48,256]{2,1,0:T(8,128)S(1)} reshape(f32[8,3,16,16,16]{4,3,2,1,0:T(8,128)} %copy.17) | data formatting | bytes 786432 | tf_op jit(solution)/shard_map/reshape | solution.py:483
  110.3 1.0 multiply_add_fusion.2
  111.5 1.0 multiply_add_fusion.1
  112.8 1.0 multiply_add_fusion
  114.0 0.9 multiply_add_fusion.3
  115.1 0.7 copy.21
  115.8 10.4 %exchange.1 = f32[4,8,16,64]{3,2,1,0:T(8,128)} custom-call(f32[4,8,16,64]{3,2,1,0:T(8,128)} %bitcast.31), custom_call_target="tpu_custom_call" | custom-call | tf_op jit(solution)/shard_map/exchange/pallas_call | solution.py:429
  126.2 1.7 %copy.23 = f32[32,16,64]{2,1,0:T(8,128)} copy(f32[32,16,64]{2,1,0:T(8,128)} %bitcast.32) | data formatting | bytes 262144
  (30 shorter events, 1.3 us)
Async XLA Ops:
  39.5 30.8 %copy-start.2 = (f32[3,4,4,16,64]{4,3,2,1,0:T(8,128)S(1)}, f32[3,4,4,16,64]{4,3,2,1,0:T(8,128)}, u32[]{:S(2)}) copy-start(f32[3,4,4,16,64]{4,3,2,1,0:T(8,128)} %get-tuple-element.10) | copy-start | bytes 589828
  70.9 1.2 copy-start
  70.9 1.8 %copy-start.1 = (f32[24,256]{1,0:T(8,128)}, f32[24,256]{1,0:T(8,128)S(1)}, u32[]{:S(2)}) copy-start(f32[24,256]{1,0:T(8,128)S(1)} %get-tuple-element.46) | copy-start | bytes 73732
